TPU v7x, 256 devices: a whole 4x4x8 slice. The times are simulated.
256 devices in a mesh: seq: 32 (over x, z_hi, y), tp: 8 (over z_lo, core).
Axes of the slice: x: 4, y: 4, z: 8 (z_hi: 2, z_lo: 4; z = z_hi * 4 + z_lo), core: 2. Of those that a mesh axis runs over, the one named last changes fastest.
Arguments:
- latent: bfloat16 [2, 32, 1024, 1152], P(None, 'seq', 'tp'), may hold values from -6 to 6
- modulation: float32 [2, 9, 1152], replicated, may hold values from -4 to 4
- qkv_spatial: bfloat16 [3, 1152, 1152], P(None, None, 'tp'), may hold values from -0.1875 to 0.1875
- gain_spatial: float32 [2, 72], replicated, may hold values from 0.5 to 1.7
- out_spatial: bfloat16 [1152, 1152], P('tp'), may hold values from -0.1875 to 0.1875
- qkv_temporal: bfloat16 [3, 1152, 1152], P(None, None, 'tp'), may hold values from -0.1875 to 0.1875
- gain_temporal: float32 [2, 72], replicated, may hold values from 0.5 to 1.7
- out_temporal: bfloat16 [1152, 1152], P('tp'), may hold values from -0.1875 to 0.1875
- fc_in: bfloat16 [1152, 4608], P(None, 'tp'), may hold values from -0.1875 to 0.1875
- fc_out: bfloat16 [4608, 1152], P('tp'), may hold values from -0.09375 to 0.09375
Outputs:
- result: bfloat16 [2, 32, 1024, 1152], P(None, 'seq', 'tp')
All inputs are finite; a program needn't handle non-finite values.
Results may differ from a plain program's by a relative error of at most 0.017.
Values may be sent and summed in bfloat16 or wider, within the bound.
A program may use at most 64 MiB of HBM per device.

v0:
```python
import math
import jax
import jax.numpy as jnp
from jax import lax
from jax.sharding import PartitionSpec as P

D = 1152
H = 16
epsilon = 1e-06


def layer_norm(values):
    average = jnp.mean(values, axis=-1, keepdims=True)
    centred = values - average
    variance = jnp.mean(centred * centred, axis=-1, keepdims=True)
    return centred * lax.rsqrt(variance + epsilon)


def modulated(field, modulation, offset):
    shift_row = modulation[:, offset][:, None, None, :]
    scale_row = modulation[:, offset + 1][:, None, None, :]
    return (layer_norm(field) * (1.0 + scale_row) + shift_row).astype(jnp.bfloat16)


def project_heads(rows_piece, table, gains, head_dim):
    results = []
    for which_part in range(3):
        projected = jnp.einsum(
            "bfpd,de->bfpe", rows_piece, table[which_part], preferred_element_type=jnp.float32
        )
        if which_part < 2:
            shaped = projected.reshape(
                projected.shape[:-1] + (projected.shape[-1] // head_dim, head_dim)
            )
            shaped = (
                shaped
                * lax.rsqrt(jnp.mean(shaped * shaped, axis=-1, keepdims=True) + epsilon)
                * gains[which_part]
            )
            projected = shaped.reshape(projected.shape)
        results.append(projected.astype(jnp.bfloat16))
    return jnp.stack(results)


def attend(query_rows, key_rows, value_rows, head_dim):
    groups, length, feature_width = query_rows.shape
    head_count = feature_width // head_dim
    query_heads = query_rows.reshape(groups, length, head_count, head_dim)
    key_heads = key_rows.reshape(groups, length, head_count, head_dim)
    value_heads = value_rows.reshape(groups, length, head_count, head_dim)
    block_rows = min(length, 512)

    def one_block(first_row):
        query_block = lax.dynamic_slice_in_dim(query_heads, first_row, block_rows, 1)
        scores = jnp.einsum(
            "gqhe,gkhe->ghqk", query_block, key_heads, preferred_element_type=jnp.float32
        ) / math.sqrt(head_dim)
        weights = jnp.exp(scores)
        probabilities = (weights / jnp.sum(weights, axis=-1, keepdims=True)).astype(jnp.bfloat16)
        return jnp.einsum(
            "ghqk,gkhe->gqhe", probabilities, value_heads, preferred_element_type=jnp.float32
        ).astype(jnp.bfloat16)

    starts = jnp.arange(length // block_rows, dtype=jnp.int32) * block_rows
    pieces = lax.map(one_block, starts)
    return pieces.transpose(1, 0, 2, 3, 4).reshape(groups, length, feature_width)


def frame_attention(query_rows, key_rows, value_rows, head_dim):
    batches, frames, patches, feature_width = query_rows.shape
    members = [
        item.transpose(0, 2, 1, 3).reshape(batches * patches, frames, feature_width)
        for item in (query_rows, key_rows, value_rows)
    ]
    mixed_heads = attend(members[0], members[1], members[2], head_dim)
    return mixed_heads.reshape(batches, patches, frames, feature_width).transpose(0, 2, 1, 3)


def body(
    latent,
    modulation,
    qkv_spatial,
    gain_spatial,
    out_spatial,
    qkv_temporal,
    gain_temporal,
    out_temporal,
    fc_in,
    fc_out,
):
    head_dim = D // H
    running = latent.astype(jnp.float32)
    normed = modulated(running, modulation, 0)
    packed = project_heads(
        lax.all_gather(normed, "tp", axis=2, tiled=True), qkv_spatial, gain_spatial, head_dim
    )
    batches, frames, patches, local_width = packed.shape[1:]
    mixed_heads = attend(
        packed[0].reshape(batches * frames, patches, local_width),
        packed[1].reshape(batches * frames, patches, local_width),
        packed[2].reshape(batches * frames, patches, local_width),
        head_dim,
    )
    mixed_heads = mixed_heads.reshape(batches, frames, patches, local_width)
    partial_value = jnp.einsum(
        "bfpe,ed->bfpd", mixed_heads, out_spatial, preferred_element_type=jnp.float32
    )
    spatial_out = lax.psum_scatter(
        partial_value.astype(jnp.bfloat16), "tp", scatter_dimension=2, tiled=True
    )
    running = running + modulation[:, 2][:, None, None, :] * spatial_out.astype(jnp.float32)
    normed = modulated(running, modulation, 3)
    moved_rows = lax.all_to_all(normed, "seq", split_axis=2, concat_axis=1, tiled=True)
    packed = project_heads(
        lax.all_gather(moved_rows, "tp", axis=2, tiled=True), qkv_temporal, gain_temporal, head_dim
    )
    mixed_heads = frame_attention(packed[0], packed[1], packed[2], head_dim)
    partial_value = jnp.einsum(
        "bfpe,ed->bfpd", mixed_heads, out_temporal, preferred_element_type=jnp.float32
    )
    shares = lax.psum_scatter(
        partial_value.astype(jnp.bfloat16), "tp", scatter_dimension=2, tiled=True
    )
    temporal_out = lax.all_to_all(shares, "seq", split_axis=1, concat_axis=2, tiled=True)
    running = running + modulation[:, 5][:, None, None, :] * temporal_out.astype(jnp.float32)
    normed = modulated(running, modulation, 6)
    projected = jnp.einsum(
        "bfpd,de->bfpe",
        lax.all_gather(normed, "tp", axis=2, tiled=True),
        fc_in,
        preferred_element_type=jnp.float32,
    )
    hidden = jax.nn.gelu(projected, approximate=True).astype(jnp.bfloat16)
    partial_value = jnp.einsum("bfpe,ed->bfpd", hidden, fc_out, preferred_element_type=jnp.float32)
    mlp_out = lax.psum_scatter(
        partial_value.astype(jnp.bfloat16), "tp", scatter_dimension=2, tiled=True
    )
    return (running + modulation[:, 8][:, None, None, :] * mlp_out.astype(jnp.float32)).astype(
        jnp.bfloat16
    )


def solution(mesh):
    placed = (
        P(None, "seq", "tp", None),
        P(),
        P(None, None, "tp"),
        P(),
        P("tp", None),
        P(None, None, "tp"),
        P(),
        P("tp", None),
        P(None, "tp"),
        P("tp", None),
    )
    return jax.shard_map(
        body, mesh=mesh, in_specs=placed, out_specs=P(None, "seq", "tp", None), check_vma=False
    )
```

profile of v0, /device:TPU:4, one launch (start us, length us, event | category | flops | bytes accessed | tf_op | source)
XLA Modules:
  0.0 529.5 jit_solution(16318409083778460695)
XLA Ops:
  6.5 0.9 slice_bitcast_fusion.1
  7.5 1.2 convert_reduce_fusion
  8.7 1.4 fusion.58
  10.1 2.2 fusion.61
  12.6 62.3 %all-gather.4.cloned.1.call-done = bf16[2,1,1024,1152]{3,2,0,1:T(8,128)(2,1)} async-done(((bf16[2,1,128,1152]{3,2,0,1:T(8,128)(2,1)}), bf16[2,1,1024,1152]{3,2,0,1:T(8,128)(2,1)}) %all-gather.4.cloned.1.call-update) | async-done | bytes 4718608 | tf_op jit(solution)/shard_map/all_gather | solution.py:95
  74.8 5.1 fusion.93
  79.9 1.4 reduce_sum.111
  81.3 5.5 %fusion.94 = (f32[2,1024,144]{1,2,0:T(8,128)}, f32[2,1024,144]{1,2,0:T(8,128)}) fusion(bf16[3,1152,144]{1,2,0:T(8,128)(2,1)} %param.14, bf16[2,1,1024,1152]{3,2,0,1:T(8,128)(2,1)} %all-gather.4.cloned.1.call-done), kind=kOutput, calls=%fused_computation.130 | convolution fusion | flops 679772160 | bytes 7409664 | tf_op jit(solution)/shard_map/bfpd,de->bfpe/dot_general | solution.py:28
  86.8 1.4 reduce_sum.112
  88.4 1.0 copy-done.4
  89.7 4.9 fusion.55
  94.6 12.8 %while.2 = (s32[]{:T(128)}, bf16[2,2,512,2,72]{2,4,3,1,0:T(8,128)(2,1)S(1)}, s32[2]{0:T(128)S(1)}, bf16[2,1024,2,72]{1,3,2,0:T(8,128)(2,1)S(1)}, bf16[2,1024,2,7...) while((s32[]{:T(128)}, ...), condition=%wide.region_6.7_spmd, body=%wide.region_4.6_spmd.sunk | while | flops 614610944 | bytes 20922552 | solution.py:65
  97.2 1.9 fusion.108
  99.1 1.9 fusion.109
  103.6 1.9 fusion.108
  105.5 1.9 fusion.109
  108.5 3.7 fusion.27
  112.3 58.9 %reduce-scatter.4.cloned.1.call-done = bf16[2,1,128,1152]{3,2,0,1:T(8,128)(2,1)} async-done(((bf16[2,1,1024,1152]{3,2,0,1:T(8,128)(2,1)}), bf16[2,1,128,1152]{3,2,0,1:T(8,128)(2,1)}) %reduce-scatter.4.cloned.1.call-update) | async-done | bytes 589840 | tf_op jit(solution)/shard_map/reduce_scatter | solution.py:108
  171.2 1.4 fusion.73
  172.6 1.4 multiply_reduce_fusion.3
  175.1 27.1 %all_to_all.21 = bf16[2,1,128,1152]{3,0,1,2:T(2,128)(2,1)S(1)} all-to-all(bf16[2,1,128,1152]{3,0,1,2:T(2,128)(2,1)S(1)} %copy.73), channel_id=1, replica_groups=mesh['seq'=32,'tp'=8] {'seq'}, dimensions={2} | all-to-all | bytes 1179648 | tf_op jit(solution)/shard_map/all_to_all | solution.py:113
  204.2 56.9 %all-gather.6.cloned.1.call-done = bf16[2,32,32,1152]{3,1,0,2:T(8,128)(2,1)} async-done(((bf16[2,32,4,1152]{3,1,0,2:T(8,128)(2,1)}), bf16[2,32,32,1152]{3,1,0,2:T(8,128)(2,1)}) %all-gather.6.cloned.1.call-update) | async-done | bytes 4718608 | tf_op jit(solution)/shard_map/all_gather | solution.py:115
  261.0 3.9 fusion.49
  265.0 1.4 reshape_reshape.10
  266.4 3.7 multiply_reduce_fusion
  270.1 3.7 multiply_reduce_fusion.1
  273.8 2.4 multiply_convert_fusion
  276.3 1.2 copy.80
  277.4 1.5 convert_element_type.119
  278.9 1.8 copy.81
  280.7 1.4 reshape_reshape.12
  282.1 2.4 copy.77
  284.5 1.5 convert_element_type.117
  286.0 1.8 copy.78
  287.8 1.4 reshape_reshape.11
  289.3 2.4 fusion.38
  292.4 1.1 copy.86
  293.5 1.5 reshape_reshape_transpose.3
  295.0 3.3 convolution_convert_fusion.1
  298.2 3.8 copy.88
  302.1 58.9 %reduce-scatter.6.cloned.1.call-done = bf16[2,32,4,1152]{3,1,0,2:T(8,128)(2,1)} async-done(((bf16[2,32,32,1152]{3,1,0,2:T(8,128)(2,1)}), bf16[2,32,4,1152]{3,1,0,2:T(8,128)(2,1)}) %reduce-scatter.6.cloned.1.call-update) | async-done | bytes 589840 | tf_op jit(solution)/shard_map/reduce_scatter | solution.py:121
  360.9 1.5 copy.89
  362.4 27.1 %all_to_all.22 = bf16[2,32,4,1152]{3,2,0,1:T(4,128)(2,1)S(1)} all-to-all(bf16[2,32,4,1152]{3,2,0,1:T(4,128)(2,1)S(1)} %copy.89), channel_id=1, replica_groups=mesh['seq'=32,'tp'=8] {'seq'}, dimensions={1} | all-to-all | bytes 1179648 | tf_op jit(solution)/shard_map/all_to_all | solution.py:124
  391.3 1.1 add_convert_fusion.1
  392.5 57.9 %all-gather.8.cloned.1.call-done = bf16[2,1,1024,1152]{3,2,0,1:T(8,128)(2,1)} async-done(((bf16[2,1,128,1152]{3,2,0,1:T(8,128)(2,1)}), bf16[2,1,1024,1152]{3,2,0,1:T(8,128)(2,1)}) %all-gather.8.cloned.1.call-update) | async-done | bytes 4718608 | tf_op jit(solution)/shard_map/all_gather | solution.py:129
  450.4 11.3 %fusion.28 = bf16[2,1,1024,1152]{3,2,0,1:T(8,128)(2,1)} fusion(bf16[2,1,1024,1152]{3,2,0,1:T(8,128)(2,1)} %all-gather.8.cloned.1.call-done, bf16[576,1152]{1,0:T(8,128)(2,1)S(1)} %copy-done, bf16[1152,576]{0,1:T(8,128)(2,1)} %param.20), kind=kOutput, calls=%fused_computation.34 | convolution fusion | flops 5448794112 | bytes 12091392 | tf_op jit(solution)/shard_map/bfpe,ed->bfpd/dot_general | solution.py:134
  461.7 58.9 %reduce-scatter.8.cloned.1.call-done = bf16[2,1,128,1152]{3,2,0,1:T(8,128)(2,1)} async-done(((bf16[2,1,1024,1152]{3,2,0,1:T(8,128)(2,1)}), bf16[2,1,128,1152]{3,2,0,1:T(8,128)(2,1)}) %reduce-scatter.8.cloned.1.call-update) | async-done | bytes 589840 | tf_op jit(solution)/shard_map/reduce_scatter | solution.py:135
  520.6 2.0 fusion.74
  (72 shorter events, 8.6 us)
Async XLA Ops:
  6.5 443.8 %copy-start = (bf16[576,1152]{1,0:T(8,128)(2,1)S(1)}, bf16[576,1152]{1,0:T(8,128)(2,1)}, u32[]{:S(2)}) copy-start(bf16[576,1152]{1,0:T(8,128)(2,1)} %param.21) | copy-start | bytes 3981316
  6.5 5.8 %copy-start.10 = (f32[2,72]{1,0:T(2,128)S(1)}, f32[2,72]{1,0:T(2,128)}, u32[]{:S(2)}) copy-start(f32[2,72]{1,0:T(2,128)} %param.15) | copy-start | bytes 1732
  6.5 68.3 %all-gather.4.cloned.1.call-start = ((), (), s32[]{:S(2)}) async-start(), calls=%async_computation.5 | async-start | bytes 5308416 | tf_op jit(solution)/shard_map/all_gather | solution.py:95
  12.3 158.9 %reduce-scatter.4.cloned.1.call-start = ((), (), s32[]{:S(2)}) async-start(), calls=%async_computation.6 | async-start | bytes 5308416 | tf_op jit(solution)/shard_map/reduce_scatter | solution.py:108
  88.2 1.3 copy-start.4
  89.7 5.0 copy-start.6
  97.1 2.0 copy-start.12
  103.6 2.0 copy-start.12
  107.5 1.1 copy-start.8
  112.2 58.9 %copy-start.1 = (bf16[2,1,128,1152]{3,2,1,0:T(8,128)(2,1)S(1)}, bf16[2,1,128,1152]{3,2,1,0:T(8,128)(2,1)}, u32[]{:S(2)}) copy-start(bf16[2,1,128,1152]{3,2,1,0:T(8,128)(2,1)} %param.12) | copy-start | bytes 1769476
  112.3 148.8 %all-gather.6.cloned.1.call-start = ((), (), s32[]{:S(2)}) async-start(), calls=%async_computation.7 | async-start | bytes 5308416 | tf_op jit(solution)/shard_map/all_gather | solution.py:115
  171.2 2.9 copy-start.2
  174.5 28.9 %copy-start.11 = (f32[2,72]{1,0:T(2,128)S(1)}, f32[2,72]{1,0:T(2,128)}, u32[]{:S(2)}) copy-start(f32[2,72]{1,0:T(2,128)} %param.18) | copy-start | bytes 1732
  174.5 28.9 %copy-start.7 = (bf16[3,1152,144]{1,2,0:T(8,128)(2,1)S(1)}, bf16[3,1152,144]{1,2,0:T(8,128)(2,1)}, u32[]{:S(2)}) copy-start(bf16[3,1152,144]{1,2,0:T(8,128)(2,1)} %param.17) | copy-start | bytes 2985988
  203.1 157.8 %reduce-scatter.6.cloned.1.call-start = ((), (), s32[]{:S(2)}) async-start(), calls=%async_computation.8 | async-start | bytes 5308416 | tf_op jit(solution)/shard_map/reduce_scatter | solution.py:121
  289.3 2.4 copy-start.5
  292.4 2.6 copy-start.9
  302.0 148.3 %all-gather.8.cloned.1.call-start = ((), (), s32[]{:S(2)}) async-start(), calls=%async_computation.9 | async-start | bytes 5308416 | tf_op jit(solution)/shard_map/all_gather | solution.py:129
  389.5 1.1 copy-start.3
  392.4 128.2 %reduce-scatter.8.cloned.1.call-start = ((), (), s32[]{:S(2)}) async-start(), calls=%async_computation.10 | async-start | bytes 5308416 | tf_op jit(solution)/shard_map/reduce_scatter | solution.py:135
Sparse Core Ops, SparseCore 0:
  12.4 62.3 all-gather.3
  112.4 58.7 reduce-scatter.3
  203.2 57.7 all-gather.5
  302.1 58.7 reduce-scatter.5
  392.5 57.7 all-gather.7
  461.8 58.7 reduce-scatter.7
where the time goes:
time: 530 us; the launch traced here: 529 us
  waiting for transfers between devices  354 us (67%)
  matrix products  55.9 us (11%)
  blocking collectives  54.2 us (10%)
  local copies, waits for them, and re-layouts  28.9 us (5%)
  other arithmetic  18.6 us (4%)
  between operations  13.8 us (3%)
    reduce_scatter x3, waiting for transfers between devices, body(): lax.psum_scatter(partial_value.astype(jnp.bfloat16), 'tp', scatter_dimens...  177 us
    all_gather x2, waiting for transfers between devices, body(): lax.all_gather(normed, 'tp', axis=2, tiled=True)  120 us
    all_gather x1, waiting for transfers between devices, body(): lax.all_gather(moved_rows, 'tp', axis=2, tiled=True)  56.9 us
    all_to_all x1, blocking collectives, body(): lax.all_to_all(normed, 'seq', split_axis=2, concat_axis=1, tiled=True)  27.1 us
    all_to_all x1, blocking collectives, body(): lax.all_to_all(shares, 'seq', split_axis=1, concat_axis=2, tiled=True)  27.1 us
    dot_general x6, matrix products, project_heads(): jnp.einsum('bfpd,de->bfpe', rows_piece, table[which_part], preferred_elem...  26.8 us
    dot_general x1, matrix products, body(): jnp.einsum('bfpe,ed->bfpd', hidden, fc_out, preferred_element_type=jnp.fl...  11.3 us
  transfers between devices with their start and end apart: 6, of which 6 were waited for; matrix products, arithmetic and copies ran while one was open for 0% of the time, Pallas kernels for 0%

commit v1 on v0

--- a/solution.py
+++ b/solution.py
@@ -126,7 +126,9 @@
     normed = modulated(running, modulation, 6)
     projected = jnp.einsum(
         "bfpd,de->bfpe",
-        lax.all_gather(normed, "tp", axis=2, tiled=True),
+        jnp.concatenate(
+            lax.all_to_all(jnp.stack([normed] * lax.axis_size("tp")), "tp", 0, 0), axis=2
+        ),
         fc_in,
         preferred_element_type=jnp.float32,
     )

time: 530 us -> 582 us (1.098)
  blocking collectives: 54.2 us -> 164 us
  waiting for transfers between devices: 354 us -> 293 us
    all_to_all x0 -> x1, blocking collectives: none -> 110 us  [body(): lax.all_to_all(jnp.stack([normed] * lax.axis_size('tp')), 'tp', 0, 0)]
    all_gather x2 -> x1, waiting for transfers between devices: 120 us -> 62.3 us  [body(): lax.all_gather(normed, 'tp', axis=2, tiled=True)]
  transfers between devices with their start and end apart: 6 -> 5, of which waited for: 6 -> 5; matrix products, arithmetic and copies ran while one was open for 0% -> 0% of each run, Pallas kernels for 0% -> 0%
where the time goes in v1:
time: 582 us; the launch traced here: 581 us
  waiting for transfers between devices  293 us (50%)
  blocking collectives  164 us (28%)
  matrix products  55.9 us (10%)
  local copies, waits for them, and re-layouts  32.2 us (6%)
  other arithmetic  17.8 us (3%)
  between operations  13.5 us (2%)
    reduce_scatter x3, waiting for transfers between devices, body(): lax.psum_scatter(partial_value.astype(jnp.bfloat16), 'tp', scatter_dimens...  174 us
    all_to_all x1, blocking collectives, body(): lax.all_to_all(jnp.stack([normed] * lax.axis_size('tp')), 'tp', 0, 0)  110 us
    all_gather x1, waiting for transfers between devices, body(): lax.all_gather(normed, 'tp', axis=2, tiled=True)  62.3 us
    all_gather x1, waiting for transfers between devices, body(): lax.all_gather(moved_rows, 'tp', axis=2, tiled=True)  56.9 us
    all_to_all x1, blocking collectives, body(): lax.all_to_all(normed, 'seq', split_axis=2, concat_axis=1, tiled=True)  27.1 us
    all_to_all x1, blocking collectives, body(): lax.all_to_all(shares, 'seq', split_axis=1, concat_axis=2, tiled=True)  27.1 us
    dot_general x6, matrix products, project_heads(): jnp.einsum('bfpd,de->bfpe', rows_piece, table[which_part], preferred_elem...  26.8 us
  transfers between devices with their start and end apart: 5, of which 5 were waited for; matrix products, arithmetic and copies ran while one was open for 0% of the time, Pallas kernels for 0%

profile of v1, /device:TPU:4, one launch (start us, length us, event | category | flops | bytes accessed | tf_op | source)
XLA Modules:
  0.0 580.9 jit_solution(8911568428961203966)
XLA Ops:
  6.5 0.9 slice_bitcast_fusion.1
  7.5 1.2 convert_reduce_fusion
  8.7 1.4 fusion.54
  10.1 2.2 fusion.57
  12.6 62.3 %all-gather.3.cloned.1.call-done = bf16[2,1,1024,1152]{3,2,0,1:T(8,128)(2,1)} async-done(((bf16[2,1,128,1152]{3,2,0,1:T(8,128)(2,1)}), bf16[2,1,1024,1152]{3,2,0,1:T(8,128)(2,1)}) %all-gather.3.cloned.1.call-update) | async-done | bytes 4718608 | tf_op jit(solution)/shard_map/all_gather | solution.py:95
  74.8 5.1 fusion.90
  79.9 1.4 reduce_sum.111
  81.3 5.5 fusion.91
  86.8 1.4 reduce_sum.112
  88.4 1.0 copy-done.4
  89.7 4.9 fusion.51
  94.6 12.8 %while.2 = (s32[]{:T(128)}, bf16[2,2,512,2,72]{2,4,3,1,0:T(8,128)(2,1)S(1)}, s32[2]{0:T(128)S(1)}, bf16[2,1024,2,72]{1,3,2,0:T(8,128)(2,1)S(1)}, bf16[2,1024,2,7...) while((s32[]{:T(128)}, ...), condition=%wide.region_6.7_spmd, body=%wide.region_4.6_spmd.sunk | while | flops 614610944 | bytes 20922552 | solution.py:65
  97.2 1.9 fusion.106
  99.1 1.9 fusion.107
  103.6 1.9 fusion.106
  105.5 1.9 fusion.107
  108.5 3.7 fusion.25
  112.3 58.9 %reduce-scatter.4.cloned.1.call-done = bf16[2,1,128,1152]{3,2,0,1:T(8,128)(2,1)} async-done(((bf16[2,1,1024,1152]{3,2,0,1:T(8,128)(2,1)}), bf16[2,1,128,1152]{3,2,0,1:T(8,128)(2,1)}) %reduce-scatter.4.cloned.1.call-update) | async-done | bytes 589840 | tf_op jit(solution)/shard_map/reduce_scatter | solution.py:108
  171.2 1.4 fusion.69
  172.6 1.4 multiply_reduce_fusion.3
  175.1 27.1 %all_to_all.26 = bf16[2,1,128,1152]{3,0,1,2:T(2,128)(2,1)S(1)} all-to-all(bf16[2,1,128,1152]{3,0,1,2:T(2,128)(2,1)S(1)} %copy.75), channel_id=1, replica_groups=mesh['seq'=32,'tp'=8] {'seq'}, dimensions={2} | all-to-all | bytes 1179648 | tf_op jit(solution)/shard_map/all_to_all | solution.py:113
  204.2 56.9 %all-gather.5.cloned.1.call-done = bf16[2,32,32,1152]{3,1,0,2:T(8,128)(2,1)} async-done(((bf16[2,32,4,1152]{3,1,0,2:T(8,128)(2,1)}), bf16[2,32,32,1152]{3,1,0,2:T(8,128)(2,1)}) %all-gather.5.cloned.1.call-update) | async-done | bytes 4718608 | tf_op jit(solution)/shard_map/all_gather | solution.py:115
  261.0 3.9 fusion.45
  265.0 1.4 reshape_reshape.10
  266.4 3.7 multiply_reduce_fusion
  270.1 3.7 multiply_reduce_fusion.1
  273.8 2.4 multiply_convert_fusion
  276.3 1.2 copy.82
  277.4 1.5 convert_element_type.121
  278.9 1.8 copy.83
  280.7 1.4 reshape_reshape.12
  282.1 2.4 copy.79
  284.5 1.5 convert_element_type.119
  286.0 1.8 copy.80
  287.8 1.4 reshape_reshape.11
  289.3 2.4 fusion.36
  292.4 1.1 copy.88
  293.5 1.5 reshape_reshape_transpose.3
  295.0 3.3 convolution_convert_fusion.1
  298.2 3.8 copy.90
  302.1 58.9 %reduce-scatter.6.cloned.1.call-done = bf16[2,32,4,1152]{3,1,0,2:T(8,128)(2,1)} async-done(((bf16[2,32,32,1152]{3,1,0,2:T(8,128)(2,1)}), bf16[2,32,4,1152]{3,1,0,2:T(8,128)(2,1)}) %reduce-scatter.6.cloned.1.call-update) | async-done | bytes 589840 | tf_op jit(solution)/shard_map/reduce_scatter | solution.py:121
  360.9 1.5 copy.91
  362.4 27.1 %all_to_all.27 = bf16[2,32,4,1152]{3,2,0,1:T(4,128)(2,1)S(1)} all-to-all(bf16[2,32,4,1152]{3,2,0,1:T(4,128)(2,1)S(1)} %copy.91), channel_id=1, replica_groups=mesh['seq'=32,'tp'=8] {'seq'}, dimensions={1} | all-to-all | bytes 1179648 | tf_op jit(solution)/shard_map/all_to_all | solution.py:124
  392.2 110.3 %all_to_all.28 = bf16[8,2,1,128,1152]{4,3,1,2,0:T(8,128)(2,1)S(1)} all-to-all(bf16[8,2,1,128,1152]{4,3,1,2,0:T(8,128)(2,1)S(1)} %stack.2), channel_id=1, replica_groups=mesh['seq'=32,'tp'=8] {'tp'}, dimensions={0} | all-to-all | bytes 9437184 | tf_op jit(solution)/shard_map/all_to_all | solution.py:130
  502.5 2.6 copy.95
  505.1 11.3 %fusion.26 = bf16[2,1,1024,1152]{3,2,0,1:T(8,128)(2,1)} fusion(bf16[2,1024,1152]{2,1,0:T(8,128)(2,1)} %bitcast.184, bf16[576,1152]{1,0:T(8,128)(2,1)S(1)} %copy-done, bf16[1152,576]{0,1:T(8,128)(2,1)} %param.20), kind=kOutput, calls=%fused_computation.32 | convolution fusion | flops 5448794112 | bytes 12091392 | tf_op jit(solution)/shard_map/bfpe,ed->bfpd/dot_general | solution.py:136
  516.4 55.9 %reduce-scatter.8.cloned.1.call-done = bf16[2,1,128,1152]{3,2,0,1:T(8,128)(2,1)} async-done(((bf16[2,1,1024,1152]{3,2,0,1:T(8,128)(2,1)}), bf16[2,1,128,1152]{3,2,0,1:T(8,128)(2,1)}) %reduce-scatter.8.cloned.1.call-update) | async-done | bytes 589840 | tf_op jit(solution)/shard_map/reduce_scatter | solution.py:137
  572.4 2.0 fusion.71
  (72 shorter events, 9.5 us)
Async XLA Ops:
  6.5 498.6 %copy-start = (bf16[576,1152]{1,0:T(8,128)(2,1)S(1)}, bf16[576,1152]{1,0:T(8,128)(2,1)}, u32[]{:S(2)}) copy-start(bf16[576,1152]{1,0:T(8,128)(2,1)} %param.21) | copy-start | bytes 3981316
  6.5 5.8 %copy-start.10 = (f32[2,72]{1,0:T(2,128)S(1)}, f32[2,72]{1,0:T(2,128)}, u32[]{:S(2)}) copy-start(f32[2,72]{1,0:T(2,128)} %param.15) | copy-start | bytes 1732
  6.5 68.3 %all-gather.3.cloned.1.call-start = ((), (), s32[]{:S(2)}) async-start(), calls=%async_computation.6 | async-start | bytes 5308416 | tf_op jit(solution)/shard_map/all_gather | solution.py:95
  12.3 158.9 %reduce-scatter.4.cloned.1.call-start = ((), (), s32[]{:S(2)}) async-start(), calls=%async_computation.7 | async-start | bytes 5308416 | tf_op jit(solution)/shard_map/reduce_scatter | solution.py:108
  88.2 1.3 copy-start.4
  89.7 5.0 copy-start.6
  97.1 2.0 copy-start.12
  103.6 2.0 copy-start.12
  107.5 1.1 copy-start.8
  112.2 58.9 %copy-start.1 = (bf16[2,1,128,1152]{3,2,1,0:T(8,128)(2,1)S(1)}, bf16[2,1,128,1152]{3,2,1,0:T(8,128)(2,1)}, u32[]{:S(2)}) copy-start(bf16[2,1,128,1152]{3,2,1,0:T(8,128)(2,1)} %param.12) | copy-start | bytes 1769476
  112.3 148.8 %all-gather.5.cloned.1.call-start = ((), (), s32[]{:S(2)}) async-start(), calls=%async_computation.8 | async-start | bytes 5308416 | tf_op jit(solution)/shard_map/all_gather | solution.py:115
  171.2 2.9 copy-start.2
  174.5 28.9 %copy-start.11 = (f32[2,72]{1,0:T(2,128)S(1)}, f32[2,72]{1,0:T(2,128)}, u32[]{:S(2)}) copy-start(f32[2,72]{1,0:T(2,128)} %param.18) | copy-start | bytes 1732
  174.5 28.9 %copy-start.7 = (bf16[3,1152,144]{1,2,0:T(8,128)(2,1)S(1)}, bf16[3,1152,144]{1,2,0:T(8,128)(2,1)}, u32[]{:S(2)}) copy-start(bf16[3,1152,144]{1,2,0:T(8,128)(2,1)} %param.17) | copy-start | bytes 2985988
  203.1 157.8 %reduce-scatter.6.cloned.1.call-start = ((), (), s32[]{:S(2)}) async-start(), calls=%async_computation.9 | async-start | bytes 5308416 | tf_op jit(solution)/shard_map/reduce_scatter | solution.py:121
  289.3 2.4 copy-start.5
  292.4 2.6 copy-start.9
  302.0 270.4 %reduce-scatter.8.cloned.1.call-start = ((), (), s32[]{:S(2)}) async-start(), calls=%async_computation.10 | async-start | bytes 5308416 | tf_op jit(solution)/shard_map/reduce_scatter | solution.py:137
  389.5 1.1 copy-start.3
Sparse Core Ops, SparseCore 0:
  12.4 62.3 all-gather.2
  112.4 58.7 reduce-scatter.3
  203.2 57.7 all-gather.4
  302.1 58.7 reduce-scatter.5
  516.5 55.7 reduce-scatter.7
